TPU v7x, 32 devices: a whole 2x2x4 slice. The times are simulated.
32 devices in a mesh: replica: 16 (over z, y, core), model: 2 (over x).
Axes of the slice: x: 2, y: 2, z: 4, core: 2. Of those that a mesh axis runs over, the one named last changes fastest.
Arguments:
- layer_grads: bfloat16 [16, 2, 4096, 1024], P('replica', None, 'model'), may hold values from -6 to 6
- last_basis: float32 [2, 1024, 32], replicated, may hold values from -6 to 6
- layer_weights: float32 [2, 4096, 1024], P(None, 'model', 'replica'), may hold values from -0.1875 to 0.1875
- momentum: float32 [2, 4096, 1024], P(None, 'model', 'replica'), may hold values from -0.3125 to 0.3125
Outputs:
- new_weights: float32 [2, 4096, 1024], P(None, 'model', 'replica')
- new_basis: float32 [2, 1024, 32], replicated
- new_momentum: float32 [2, 4096, 1024], P(None, 'model', 'replica')
All inputs are finite; a program needn't handle non-finite values.
Results may differ from a plain program's by a relative error of at most 0.0029.
Values sent between devices are 32-bit elements; how exact they have to be, the bound alone decides.
A program may use at most 64 MiB of HBM per device.

v0:
```python
import jax
import jax.numpy as jnp
from jax import lax
from jax.sharding import PartitionSpec as P

RANK = 32


def shards(layer_grads, last_basis, layer_weights, momentum):
    own_grads = layer_grads[0]
    part_left = jnp.einsum(
        "liw,lwr->lir",
        own_grads,
        last_basis.astype(jnp.bfloat16),
        preferred_element_type=jnp.float32,
    )
    shares = lax.psum_scatter(part_left, "replica", scatter_dimension=1, tiled=True)
    left = lax.all_gather(shares, "replica", axis=1, tiled=True)
    part_gram = jnp.einsum("lir,lis->lrs", left, left, precision=lax.Precision.HIGHEST)
    small_left = left.astype(jnp.bfloat16)
    gram = lax.psum(part_gram, "model")
    part_right = jnp.einsum(
        "liw,lir->lwr", own_grads, small_left, preferred_element_type=jnp.float32
    )
    right = lax.psum(part_right, ("replica", "model"))
    gram = gram + 0.001 * jnp.mean(jnp.diagonal(gram, axis1=1, axis2=2), axis=1)[
        :, None, None
    ] * jnp.eye(RANK, dtype=jnp.float32)
    place = lax.axis_index("replica") * layer_weights.shape[2]
    own_right = lax.dynamic_slice_in_dim(right, place, layer_weights.shape[2], axis=1)
    root = jnp.linalg.cholesky(gram)
    half = lax.linalg.triangular_solve(
        root, jnp.swapaxes(own_right, 1, 2), left_side=True, lower=True
    )
    mixed = lax.linalg.triangular_solve(root, half, left_side=True, lower=True, transpose_a=True)
    change = jnp.einsum(
        "lir,lrw->liw", left, mixed, precision=lax.Precision.HIGHEST
    ) / lax.axis_size("replica")
    new_momentum = 0.9 * momentum + change
    new_weights = layer_weights - 0.02 * new_momentum
    new_basis = right * lax.rsqrt(jnp.mean(right * right, axis=(1, 2), keepdims=True) + 1e-12)
    return (new_weights, new_basis, new_momentum)


def solution(mesh):
    in_specs = (
        P("replica", None, "model", None),
        P(),
        P(None, "model", "replica"),
        P(None, "model", "replica"),
    )
    out_specs = (P(None, "model", "replica"), P(), P(None, "model", "replica"))
    return jax.shard_map(shards, mesh=mesh, in_specs=in_specs, out_specs=out_specs, check_vma=False)
```

profile of v0, /device:TPU:0, one launch (start us, length us, event | category | flops | bytes accessed | tf_op | source)
XLA Modules:
  0.0 245.5 jit_solution(10136461796317535133)
XLA Ops:
  7.2 0.0 reduce-scatter.2.cloned.1.call-start
  7.2 6.7 %fusion.2 = f32[2,2048,32]{1,2,0:T(8,128)} fusion(bf16[1,2,2048,1024]{3,2,1,0:T(8,128)(2,1)} %param.4, f32[2,1024,32]{1,2,0:T(8,128)} %param.5), kind=kOutput, calls=%fused_computation.3 | convolution fusion | flops 268500992 | bytes 9175040 | tf_op jit(solution)/shard_map/liw,lwr->lir/dot_general | solution.py:11
  14.0 0.0 all-reduce.2.cloned.1.call-start
  14.0 0.1 copy.13
  14.2 58.9 %reduce-scatter.2.cloned.1.call-done = f32[2,128,32]{1,2,0:T(8,128)} async-done(((f32[2,2048,32]{1,2,0:T(8,128)}), f32[2,128,32]{1,2,0:T(8,128)}) %reduce-scatter.2.cloned.1.call-update) | async-done | bytes 32784 | tf_op jit(solution)/shard_map/reduce_scatter | solution.py:17
  73.1 21.1 %all_gather.3 = f32[2,2048,32]{1,2,0:T(8,128)S(1)} all-gather(f32[2,128,32]{1,2,0:T(8,128)} %reduce-scatter.2.cloned.1.call-done), channel_id=1, replica_groups=mesh['replica'=16,'model'=2] {'replica'}, dimensions={1}, use_global_device_ids=true | all-gather | bytes 557056 | tf_op jit(solution)/shard_map/all_gather | solution.py:18
  94.1 0.6 fusion.18
  94.7 5.8 %fusion.5 = f32[2,1024,32]{1,2,0:T(8,128)} fusion(bf16[1,2,2048,1024]{3,2,1,0:T(8,128)(2,1)} %param.4, f32[2,2048,32]{1,2,0:T(8,128)S(1)} %all_gather.3), kind=kOutput, calls=%fused_computation.7 | convolution fusion | flops 268566528 | bytes 9175040 | tf_op jit(solution)/shard_map/liw,lir->lwr/dot_general | solution.py:22
  100.5 8.3 %psum.14 = f32[2,32,32]{1,2,0:T(8,128)S(1)} all-reduce(f32[2,32,32]{1,2,0:T(8,128)S(1)} %fusion.18), channel_id=1, replica_groups=mesh['replica'=16,'model'=2] {'model'}, use_global_device_ids=true, to_apply=%region_1.0 | all-reduce | flops 2048 | bytes 16384 | tf_op jit(solution)/shard_map/psum | solution.py:21
  108.9 0.6 copy.12
  109.4 0.7 gather_fusion
  110.2 0.1 multiply_add_fusion
  110.2 0.1 copy.14
  110.3 0.1 fusion.14
  110.4 5.9 %custom-call.9 = f32[2,32,32]{2,1,0:T(8,128)S(1)} custom-call(f32[2,32,32]{2,1,0:T(8,128)S(1)} %fusion.14), custom_call_target="Cholesky" | custom-call | tf_op jit(solution)/shard_map/jit(cholesky)/cholesky | solution.py:31
  116.3 0.1 compare_reduce_fusion
  116.4 0.1 select_bitcast_fusion
  116.5 4.9 %custom-call.10 = f32[2,1,32,32]{2,3,1,0:T(8,128)S(1)} custom-call(f32[2,1,32,32]{3,2,1,0:T(8,128)S(1)} %select_bitcast_fusion), custom_call_target="InvertDiagBlocksLowerTriangular" | custom-call | tf_op jit(solution)/shard_map/triangular_solve | solution.py:35
  121.4 110.8 %all-reduce.2.cloned.1.call-done = f32[2,1024,32]{1,2,0:T(8,128)} async-done(((f32[2,1024,32]{1,2,0:T(8,128)}), f32[2,1024,32]{1,2,0:T(8,128)}) %all-reduce.2.cloned.1.call-update) | async-done | bytes 262160 | tf_op jit(solution)/shard_map/psum | solution.py:25
  232.1 1.1 multiply_reduce_fusion
  233.2 1.0 fusion.12
  234.3 0.2 fusion.10
  234.4 2.5 %multiply_subtract_fusion = (f32[2,2048,64]{1,2,0:T(8,128)}, f32[2,2048,64]{1,2,0:T(8,128)}) fusion(f32[2,2048,64]{1,2,0:T(8,128)S(1)} %copy-done, f32[2,2048,32]{1,2,0:T(8,128)S(1)} %all_gather.3, f32[2,32,64]{2,1,0:T(8,128)S(1)} %fusion.10, f32[2,2048,64]{1,2,0:T(8,128)S(1)} %copy-done.1), kind=kOutput, calls=%fused_computation.8 | convolution fusion | flops 101974016 | bytes 4734976 | tf_op jit(solution)/shard_map/lir,lrw->liw/dot_general | solution.py:36
  236.9 1.7 broadcast_multiply_fusion
  (14 shorter events, 0.1 us)
Async XLA Ops:
  7.2 65.9 %reduce-scatter.2.cloned.1.call-start = ((), (), s32[]{:S(2)}) async-start(), calls=%async_computation.1 | async-start | bytes 557056 | tf_op jit(solution)/shard_map/reduce_scatter | solution.py:17
  14.0 218.2 %all-reduce.2.cloned.1.call-start = ((), (), s32[]{:S(2)}) async-start(), calls=%async_computation.2 | async-start | bytes 524288 | tf_op jit(solution)/shard_map/psum | solution.py:25
  94.7 139.7 %copy-start = (f32[2,2048,64]{1,2,0:T(8,128)S(1)}, f32[2,2048,64]{1,2,0:T(8,128)}, u32[]{:S(2)}) copy-start(f32[2,2048,64]{1,2,0:T(8,128)} %param.6) | copy-start | bytes 3145732
  94.7 139.7 %copy-start.1 = (f32[2,2048,64]{1,2,0:T(8,128)S(1)}, f32[2,2048,64]{1,2,0:T(8,128)}, u32[]{:S(2)}) copy-start(f32[2,2048,64]{1,2,0:T(8,128)} %param.7) | copy-start | bytes 3145732
Sparse Core Ops, SparseCore 0:
  14.1 58.9 reduce-scatter.1
  109.0 123.1 all-reduce.1
where the time goes:
time: 246 us
  waiting for transfers between devices  170 us (69%)
  blocking collectives  29.4 us (12%)
  matrix products  16.8 us (7%)
  between operations  14.1 us (6%)
  other arithmetic  14 us (6%)
    psum x1, waiting for transfers between devices, shards(): right = lax.psum(part_right, ('replica', 'model'))  111 us
    reduce_scatter x1, waiting for transfers between devices, shards(): lax.psum_scatter(part_left, 'replica', scatter_dimension=1, tiled=True)  58.9 us
    all_gather x1, blocking collectives, shards(): left = lax.all_gather(shares, 'replica', axis=1, tiled=True)  21.1 us
    psum x1, blocking collectives, shards(): gram = lax.psum(part_gram, 'model')  8.32 us
    dot_general x1, matrix products, shards(): jnp.einsum('liw,lwr->lir', own_grads, last_basis.astype(jnp.bfloat16), pr...  6.75 us
    another operation x4, other arithmetic, shards(): root = jnp.linalg.cholesky(gram)  6.01 us
    dot_general x1, matrix products, shards(): jnp.einsum('liw,lir->lwr', own_grads, small_left, preferred_element_type=...  5.78 us
    another operation x3, other arithmetic, shards(): lax.linalg.triangular_solve(root, half, left_side=True, lower=True, trans...  5 us
  transfers between devices with their start and end apart: 2, of which 2 were waited for; matrix products, arithmetic and copies ran while one was open for 5% of the time, Pallas kernels for 0%

commit v1 on v0

--- a/solution.py
+++ b/solution.py
@@ -22,7 +22,8 @@
     part_right = jnp.einsum(
         "liw,lir->lwr", own_grads, small_left, preferred_element_type=jnp.float32
     )
-    right = lax.psum(part_right, ("replica", "model"))
+    drive_panel = lambda m: jax.lax.psum(jax.lax.psum(m, "model"), "replica")
+    right = drive_panel(part_right)
     gram = gram + 0.001 * jnp.mean(jnp.diagonal(gram, axis1=1, axis2=2), axis=1)[
         :, None, None
     ] * jnp.eye(RANK, dtype=jnp.float32)

time: 246 us -> 235 us (0.955)
  waiting for transfers between devices: 170 us -> 159 us
    psum x1 -> x2, waiting for transfers between devices: 111 us -> 100 us  [shards(): drive_panel = lambda m: jax.lax.psum(jax.lax.psum(m, 'model'), 'replica')]
  transfers between devices with their start and end apart: 2 -> 3, of which waited for: 2 -> 3; matrix products, arithmetic and copies ran while one was open for 5% -> 5% of each run, Pallas kernels for 0% -> 0%
where the time goes in v1:
time: 235 us
  waiting for transfers between devices  159 us (68%)
  blocking collectives  29.4 us (13%)
  matrix products  16.8 us (7%)
  other arithmetic  14 us (6%)
  between operations  13.8 us (6%)
    psum x2, waiting for transfers between devices, shards(): drive_panel = lambda m: jax.lax.psum(jax.lax.psum(m, 'model'), 'replica')  100 us
    reduce_scatter x1, waiting for transfers between devices, shards(): lax.psum_scatter(part_left, 'replica', scatter_dimension=1, tiled=True)  58.9 us
    all_gather x1, blocking collectives, shards(): left = lax.all_gather(shares, 'replica', axis=1, tiled=True)  21.1 us
    psum x1, blocking collectives, shards(): gram = lax.psum(part_gram, 'model')  8.32 us
    dot_general x1, matrix products, shards(): jnp.einsum('liw,lwr->lir', own_grads, last_basis.astype(jnp.bfloat16), pr...  6.75 us
    another operation x4, other arithmetic, shards(): root = jnp.linalg.cholesky(gram)  6.01 us
    dot_general x1, matrix products, shards(): jnp.einsum('liw,lir->lwr', own_grads, small_left, preferred_element_type=...  5.78 us
    another operation x3, other arithmetic, shards(): lax.linalg.triangular_solve(root, half, left_side=True, lower=True, trans...  4.99 us
  transfers between devices with their start and end apart: 3, of which 3 were waited for; matrix products, arithmetic and copies ran while one was open for 5% of the time, Pallas kernels for 0%

profile of v1, /device:TPU:0, one launch (start us, length us, event | category | flops | bytes accessed | tf_op | source)
XLA Modules:
  0.0 234.8 jit_solution(10342738010447365730)
XLA Ops:
  7.2 6.7 %fusion.2 = f32[2,2048,32]{1,2,0:T(8,128)} fusion(bf16[1,2,2048,1024]{3,2,1,0:T(8,128)(2,1)} %param.4, f32[2,1024,32]{1,2,0:T(8,128)} %param.5), kind=kOutput, calls=%fused_computation.3 | convolution fusion | flops 268500992 | bytes 9175040 | tf_op jit(solution)/shard_map/liw,lwr->lir/dot_general | solution.py:11
  14.0 0.0 all-reduce.3.cloned.1.call-start
  14.0 0.1 copy.13
  14.2 58.9 %reduce-scatter.2.cloned.1.call-done = f32[2,128,32]{1,2,0:T(8,128)} async-done(((f32[2,2048,32]{1,2,0:T(8,128)}), f32[2,128,32]{1,2,0:T(8,128)}) %reduce-scatter.2.cloned.1.call-update) | async-done | bytes 32784 | tf_op jit(solution)/shard_map/reduce_scatter | solution.py:17
  73.1 21.1 %all_gather.3 = f32[2,2048,32]{1,2,0:T(8,128)S(1)} all-gather(f32[2,128,32]{1,2,0:T(8,128)} %reduce-scatter.2.cloned.1.call-done), channel_id=1, replica_groups=mesh['replica'=16,'model'=2] {'replica'}, dimensions={1}, use_global_device_ids=true | all-gather | bytes 557056 | tf_op jit(solution)/shard_map/all_gather | solution.py:18
  94.1 0.6 fusion.18
  94.7 5.8 %fusion.5 = f32[2,1024,32]{1,2,0:T(8,128)} fusion(bf16[1,2,2048,1024]{3,2,1,0:T(8,128)(2,1)} %param.4, f32[2,2048,32]{1,2,0:T(8,128)S(1)} %all_gather.3), kind=kOutput, calls=%fused_computation.7 | convolution fusion | flops 268566528 | bytes 9175040 | tf_op jit(solution)/shard_map/liw,lir->lwr/dot_general | solution.py:22
  100.5 8.3 %psum.21 = f32[2,32,32]{1,2,0:T(8,128)S(1)} all-reduce(f32[2,32,32]{1,2,0:T(8,128)S(1)} %fusion.18), channel_id=1, replica_groups=mesh['replica'=16,'model'=2] {'model'}, use_global_device_ids=true, to_apply=%region_1.0 | all-reduce | flops 2048 | bytes 16384 | tf_op jit(solution)/shard_map/psum | solution.py:21
  108.9 0.6 copy.12
  109.5 0.7 gather_fusion
  110.2 0.1 multiply_add_fusion
  110.3 0.1 copy.14
  110.4 0.1 fusion.14
  110.4 5.9 %custom-call.9 = f32[2,32,32]{2,1,0:T(8,128)S(1)} custom-call(f32[2,32,32]{2,1,0:T(8,128)S(1)} %fusion.14), custom_call_target="Cholesky" | custom-call | tf_op jit(solution)/shard_map/jit(cholesky)/cholesky | solution.py:32
  116.3 0.1 compare_reduce_fusion
  116.4 12.2 %all-reduce.3.cloned.1.call-done = f32[2,1024,32]{1,2,0:T(8,128)} async-done(((f32[2,1024,32]{1,2,0:T(8,128)}), f32[2,1024,32]{1,2,0:T(8,128)}) %all-reduce.3.cloned.1.call-update) | async-done | bytes 262160 | tf_op jit(solution)/shard_map/psum | solution.py:25
  128.6 0.1 select_bitcast_fusion
  128.7 4.9 %custom-call.10 = f32[2,1,32,32]{2,3,1,0:T(8,128)S(1)} custom-call(f32[2,1,32,32]{3,2,1,0:T(8,128)S(1)} %select_bitcast_fusion), custom_call_target="InvertDiagBlocksLowerTriangular" | custom-call | tf_op jit(solution)/shard_map/triangular_solve | solution.py:36
  133.6 88.1 %all-reduce.5.cloned.1.call-done = f32[2,1024,32]{1,2,0:T(8,128)} async-done(((f32[2,1024,32]{1,2,0:T(8,128)}), f32[2,1024,32]{1,2,0:T(8,128)}) %all-reduce.5.cloned.1.call-update) | async-done | bytes 262160 | tf_op jit(solution)/shard_map/psum | solution.py:25
  221.8 1.1 multiply_reduce_fusion
  222.8 1.0 fusion.12
  223.9 0.2 fusion.10
  224.1 2.5 %multiply_subtract_fusion = (f32[2,2048,64]{1,2,0:T(8,128)}, f32[2,2048,64]{1,2,0:T(8,128)}) fusion(f32[2,2048,64]{1,2,0:T(8,128)S(1)} %copy-done, f32[2,2048,32]{1,2,0:T(8,128)S(1)} %all_gather.3, f32[2,32,64]{2,1,0:T(8,128)S(1)} %fusion.10, f32[2,2048,64]{1,2,0:T(8,128)S(1)} %copy-done.1), kind=kOutput, calls=%fused_computation.8 | convolution fusion | flops 101974016 | bytes 4734976 | tf_op jit(solution)/shard_map/lir,lrw->liw/dot_general | solution.py:37
  226.6 1.7 broadcast_multiply_fusion
  (17 shorter events, 0.2 us)
Async XLA Ops:
  7.2 65.9 %reduce-scatter.2.cloned.1.call-start = ((), (), s32[]{:S(2)}) async-start(), calls=%async_computation.1 | async-start | bytes 557056 | tf_op jit(solution)/shard_map/reduce_scatter | solution.py:17
  14.0 114.6 %all-reduce.3.cloned.1.call-start = ((), (), s32[]{:S(2)}) async-start(), calls=%async_computation.2 | async-start | bytes 524288 | tf_op jit(solution)/shard_map/psum | solution.py:25
  94.7 129.4 %copy-start = (f32[2,2048,64]{1,2,0:T(8,128)S(1)}, f32[2,2048,64]{1,2,0:T(8,128)}, u32[]{:S(2)}) copy-start(f32[2,2048,64]{1,2,0:T(8,128)} %param.6) | copy-start | bytes 3145732
  94.7 129.4 %copy-start.1 = (f32[2,2048,64]{1,2,0:T(8,128)S(1)}, f32[2,2048,64]{1,2,0:T(8,128)}, u32[]{:S(2)}) copy-start(f32[2,2048,64]{1,2,0:T(8,128)} %param.7) | copy-start | bytes 3145732
  108.9 112.9 %all-reduce.5.cloned.1.call-start = ((), (), s32[]{:S(2)}) async-start(), calls=%async_computation.3 | async-start | bytes 524288 | tf_op jit(solution)/shard_map/psum | solution.py:25
Sparse Core Ops, SparseCore 0:
  14.1 58.9 reduce-scatter.1
  109.0 19.5 all-reduce.2
  132.0 89.7 all-reduce.4

commit v2 on v0

--- a/solution.py
+++ b/solution.py
@@ -1,9 +1,18 @@
+import functools
 import jax
 import jax.numpy as jnp
 from jax import lax
 from jax.sharding import PartitionSpec as P
 
 RANK = 32
+
+
+def place_block(u, peer_axis):
+    item_now = lax.all_gather(u, peer_axis)
+    return jnp.sum(item_now, axis=0)
+
+
+_bind_knots = functools.partial(place_block, peer_axis=("replica", "model"))
 
 
 def shards(layer_grads, last_basis, layer_weights, momentum):
@@ -22,7 +31,7 @@
     part_right = jnp.einsum(
         "liw,lir->lwr", own_grads, small_left, preferred_element_type=jnp.float32
     )
-    right = lax.psum(part_right, ("replica", "model"))
+    right = _bind_knots(part_right)
     gram = gram + 0.001 * jnp.mean(jnp.diagonal(gram, axis1=1, axis2=2), axis=1)[
         :, None, None
     ] * jnp.eye(RANK, dtype=jnp.float32)

time: 246 us -> 189 us (0.77)
  waiting for transfers between devices: 170 us -> 112 us
    psum x1 -> x0, waiting for transfers between devices: 111 us -> none  [shards(): right = lax.psum(part_right, ('replica', 'model'))]
    all_gather x0 -> x1, waiting for transfers between devices: none -> 52.8 us  [place_block(): item_now = lax.all_gather(u, peer_axis)]
    reduce_sum x0 -> x1, other arithmetic: none -> 3.98 us  [place_block(): return jnp.sum(item_now, axis=0)]
  transfers between devices with their start and end apart: 2 -> 2, of which waited for: 2 -> 2; matrix products, arithmetic and copies ran while one was open for 5% -> 7% of each run, Pallas kernels for 0% -> 0%
where the time goes in v2:
time: 189 us
  waiting for transfers between devices  112 us (59%)
  blocking collectives  29.5 us (16%)
  other arithmetic  16.1 us (9%)
  matrix products  15.9 us (8%)
  between operations  14.1 us (7%)
    reduce_scatter x1, waiting for transfers between devices, shards(): lax.psum_scatter(part_left, 'replica', scatter_dimension=1, tiled=True)  59 us
    all_gather x1, waiting for transfers between devices, place_block(): item_now = lax.all_gather(u, peer_axis)  52.8 us
    all_gather x1, blocking collectives, shards(): left = lax.all_gather(shares, 'replica', axis=1, tiled=True)  21.1 us
    psum x1, blocking collectives, shards(): gram = lax.psum(part_gram, 'model')  8.47 us
    dot_general x1, matrix products, shards(): jnp.einsum('liw,lwr->lir', own_grads, last_basis.astype(jnp.bfloat16), pr...  6.75 us
    another operation x4, other arithmetic, shards(): root = jnp.linalg.cholesky(gram)  6.01 us
    dot_general x1, matrix products, shards(): jnp.einsum('liw,lir->lwr', own_grads, small_left, preferred_element_type=...  5.63 us
    another operation x3, other arithmetic, shards(): lax.linalg.triangular_solve(root, half, left_side=True, lower=True, trans...  5.03 us
  transfers between devices with their start and end apart: 2, of which 2 were waited for; matrix products, arithmetic and copies ran while one was open for 7% of the time, Pallas kernels for 0%

profile of v2, /device:TPU:0, one launch (start us, length us, event | category | flops | bytes accessed | tf_op | source)
XLA Modules:
  0.0 189.0 jit_solution(9224500160733540844)
XLA Ops:
  7.2 6.7 %fusion.2 = f32[2,2048,32]{1,2,0:T(8,128)} fusion(bf16[1,2,2048,1024]{3,2,1,0:T(8,128)(2,1)} %param.4, f32[2,1024,32]{1,2,0:T(8,128)} %param.5), kind=kOutput, calls=%fused_computation.3 | convolution fusion | flops 268500992 | bytes 9175040 | tf_op jit(solution)/shard_map/liw,lwr->lir/dot_general | solution.py:20
  14.0 0.0 all-gather.3.cloned.1.call-start
  14.0 59.0 %reduce-scatter.2.cloned.1.call-done = f32[2,128,32]{1,2,0:T(8,128)} async-done(((f32[2,2048,32]{1,2,0:T(8,128)}), f32[2,128,32]{1,2,0:T(8,128)}) %reduce-scatter.2.cloned.1.call-update) | async-done | bytes 32784 | tf_op jit(solution)/shard_map/reduce_scatter | solution.py:26
  73.1 21.1 %all_gather.9 = f32[2,2048,32]{1,2,0:T(8,128)S(1)} all-gather(f32[2,128,32]{1,2,0:T(8,128)} %reduce-scatter.2.cloned.1.call-done), channel_id=1, replica_groups=mesh['replica'=16,'model'=2] {'replica'}, dimensions={1}, use_global_device_ids=true | all-gather | bytes 557056 | tf_op jit(solution)/shard_map/all_gather | solution.py:27
  94.1 5.6 %fusion.5 = f32[2,1024,32]{1,2,0:T(8,128)} fusion(bf16[1,2,2048,1024]{3,2,1,0:T(8,128)(2,1)} %param.4, f32[2,2048,32]{1,2,0:T(8,128)S(1)} %all_gather.9), kind=kOutput, calls=%fused_computation.7 | convolution fusion | flops 268566528 | bytes 9175040 | tf_op jit(solution)/shard_map/liw,lir->lwr/dot_general | solution.py:31
  99.8 0.1 copy.17
  99.9 0.6 fusion.18
  100.5 8.5 %psum.7 = f32[2,32,32]{1,2,0:T(8,128)S(1)} all-reduce(f32[2,32,32]{1,2,0:T(8,128)S(1)} %fusion.18), channel_id=1, replica_groups=mesh['replica'=16,'model'=2] {'model'}, use_global_device_ids=true, to_apply=%region_1.0 | all-reduce | flops 2048 | bytes 16384 | tf_op jit(solution)/shard_map/psum | solution.py:30
  109.0 0.6 copy.16
  109.5 0.7 gather_fusion
  110.3 0.1 multiply_add_fusion
  110.3 0.1 copy.18
  110.4 0.1 fusion.14
  110.5 5.9 %custom-call.9 = f32[2,32,32]{2,1,0:T(8,128)S(1)} custom-call(f32[2,32,32]{2,1,0:T(8,128)S(1)} %fusion.14), custom_call_target="Cholesky" | custom-call | tf_op jit(solution)/shard_map/jit(cholesky)/cholesky | solution.py:40
  116.4 0.1 compare_reduce_fusion
  116.5 0.1 select_bitcast_fusion
  116.6 4.9 %custom-call.10 = f32[2,1,32,32]{2,3,1,0:T(8,128)S(1)} custom-call(f32[2,1,32,32]{3,2,1,0:T(8,128)S(1)} %select_bitcast_fusion), custom_call_target="InvertDiagBlocksLowerTriangular" | custom-call | tf_op jit(solution)/shard_map/triangular_solve | solution.py:44
  121.5 52.8 %all-gather.3.cloned.1.call-done = f32[64,1024,32]{1,2,0:T(8,128)} async-done(((f32[2,1024,32]{1,2,0:T(8,128)}), f32[64,1024,32]{1,2,0:T(8,128)}) %all-gather.3.cloned.1.call-update) | async-done | bytes 8388624 | tf_op jit(solution)/shard_map/all_gather | solution.py:11
  174.3 4.0 %reduce_sum.28 = f32[2,1024,32]{1,2,0:T(8,128)S(1)} reduce(f32[32,2,1024,32]{2,3,1,0:T(8,128)} %bitcast.28, f32[]{:T(128)} %constant.68.clone.1), dimensions={0}, to_apply=%region_5.6 | reduce | flops 2031616 | bytes 8650756 | tf_op jit(solution)/shard_map/reduce_sum | solution.py:12
  178.3 0.1 multiply_reduce_fusion
  178.4 0.3 fusion.12
  178.7 0.2 fusion.10
  178.9 0.8 broadcast_multiply_fusion
  179.6 2.5 %multiply_subtract_fusion = (f32[2,2048,64]{1,2,0:T(8,128)}, f32[2,2048,64]{1,2,0:T(8,128)}) fusion(f32[2,2048,64]{1,2,0:T(8,128)S(1)} %copy-done, f32[2,2048,32]{1,2,0:T(8,128)S(1)} %all_gather.9, f32[2,32,64]{2,1,0:T(8,128)S(1)} %fusion.10, f32[2,2048,64]{1,2,0:T(8,128)S(1)} %copy-done.1), kind=kOutput, calls=%fused_computation.8 | convolution fusion | flops 101974016 | bytes 4734976 | tf_op jit(solution)/shard_map/lir,lrw->liw/dot_general | solution.py:45
  (15 shorter events, 0.2 us)
Async XLA Ops:
  7.2 65.9 %reduce-scatter.2.cloned.1.call-start = ((), (), s32[]{:S(2)}) async-start(), calls=%async_computation.1 | async-start | bytes 557056 | tf_op jit(solution)/shard_map/reduce_scatter | solution.py:26
  14.0 160.3 %all-gather.3.cloned.1.call-start = ((), (), s32[]{:S(2)}) async-start(), calls=%async_computation.2 | async-start | bytes 8650752 | tf_op jit(solution)/shard_map/all_gather | solution.py:11
  99.8 79.9 %copy-start = (f32[2,2048,64]{1,2,0:T(8,128)S(1)}, f32[2,2048,64]{1,2,0:T(8,128)}, u32[]{:S(2)}) copy-start(f32[2,2048,64]{1,2,0:T(8,128)} %param.6) | copy-start | bytes 3145732
  99.8 79.9 %copy-start.1 = (f32[2,2048,64]{1,2,0:T(8,128)S(1)}, f32[2,2048,64]{1,2,0:T(8,128)}, u32[]{:S(2)}) copy-start(f32[2,2048,64]{1,2,0:T(8,128)} %param.7) | copy-start | bytes 3145732
Sparse Core Ops, SparseCore 0:
  14.1 58.9 reduce-scatter.1
  99.9 74.3 all-gather.2
